TPU v7x, 512 devices: a whole 4x8x8 slice. The times are simulated.
512 devices in a mesh: seq: 8 (over z), dp: 64 (over y, x, core).
Axes of the slice: x: 4, y: 8, z: 8, core: 2. Of those that a mesh axis runs over, the one named last changes fastest.
Arguments:
- accept_arrays: bfloat16 [64, 1024, 2048], P('dp', 'seq'), may hold values from -4 to 4
- lookup_arrays: bfloat16 [64, 1024, 2048], P('dp', 'seq'), may hold values from -0.75 to 0.75
- payload_arrays: bfloat16 [64, 1024, 2048], P('dp', 'seq'), may hold values from -6 to 6
- fading_exponent: bfloat16 [64, 1024, 2048], P('dp', 'seq'), may hold values from -14 to 1
- self_boost: float32 [32, 64], replicated, may hold values from -3 to 3
- result_cotangent: bfloat16 [64, 1024, 2048], P('dp', 'seq'), may hold values from -0.75 to 0.75
- initial_memory_matrix: float32 [2048, 64], replicated, may hold values from -12 to 12
Outputs:
- receptance_grad: bfloat16 [64, 1024, 2048], P('dp', 'seq')
- lookup_cotangent: bfloat16 [64, 1024, 2048], P('dp', 'seq')
- value_grad: bfloat16 [64, 1024, 2048], P('dp', 'seq')
- state_grad: float32 [2048, 64], P('dp', 'seq')
All inputs are finite; a program needn't handle non-finite values.
Results may differ from a plain program's by a relative error of at most 0.001.
Values sent between devices are 32-bit elements; how exact they have to be, the bound alone decides.
A program may use at most 128 MiB of HBM per device.

v0:
```python
import functools

import jax
import jax.numpy as jnp
from jax import lax
from jax.experimental import pallas as pl
from jax.experimental.pallas import tpu as pltpu
from jax.sharding import PartitionSpec as P

F32 = jnp.float32
BF16 = jnp.bfloat16
LANES = 128
BLOCK = 32


def dot_nn(a, b):
    return lax.dot_general(a, b, (((1,), (0,)), ((), ())), preferred_element_type=F32)


def dot_nt(a, b):
    return lax.dot_general(a, b, (((1,), (1,)), ((), ())), preferred_element_type=F32)


def dot_tn(a, b):
    return lax.dot_general(a, b, (((0,), (0,)), ((), ())), preferred_element_type=F32)


def halves(x):
    hi = x.astype(BF16)
    return hi, (x - hi.astype(F32)).astype(BF16)


def thirds(x):
    hi = x.astype(BF16)
    rest = x - hi.astype(F32)
    mid = rest.astype(BF16)
    return hi, mid, (rest - mid.astype(F32)).astype(BF16)


def iota2(shape, dim):
    return lax.broadcasted_iota(jnp.int32, shape, dim)


def per_head(x):
    first = iota2(x.shape, 1) < LANES // 2
    zero = jnp.zeros_like(x)
    return jnp.concatenate([jnp.where(first, x, zero), jnp.where(first, zero, x)], axis=0)


def per_head_halves(x):
    hi, lo = halves(per_head(x))
    return jnp.concatenate([hi, lo], axis=1)


def folded(x):
    return x[:, :LANES] + x[:, LANES:]


def rows_of(parts):
    return jnp.concatenate([jnp.broadcast_to(p, (BLOCK, LANES)) for p in parts], axis=0)


def decays(f_ref, at):
    tok = f_ref.shape[0]
    log_w = -jnp.exp(f_ref[:, at].astype(F32))
    row, col = iota2((tok, tok), 0), iota2((tok, tok), 1)
    tri = jnp.where((col <= row) & (col // BLOCK == row // BLOCK), 1.0, 0.0).astype(BF16)
    hi, mid, lo = thirds(log_w)
    sums = dot_nn(tri, jnp.concatenate([hi, mid, lo], axis=1))
    upto = sums[:, :LANES] + (sums[:, LANES : 2 * LANES] + sums[:, 2 * LANES :])
    return upto, upto - log_w


def totals_of(upto):
    return [upto[b * BLOCK + BLOCK - 1 : (b + 1) * BLOCK] for b in range(upto.shape[0] // BLOCK)]


def phase_one(i, refs):
    at = pl.ds(pl.multiple_of(i * LANES, LANES), LANES)
    upto, before = decays(refs["f"], at)
    t = totals_of(upto)
    zero = jnp.zeros_like(t[0])
    early = jnp.exp(before + rows_of([zero, t[0], t[0] + t[1], t[0] + t[1] + t[2]]))
    tail = jnp.exp(rows_of([t[0] + t[1] + t[2] + t[3], t[1] + t[2] + t[3], t[2] + t[3], t[3]]) - upto)
    refs["upto"][:, at] = upto
    refs["before"][:, at] = before
    refs["early"][:, at] = early
    refs["tail"][:, at] = tail
    refs["decay"][:, at] = jnp.exp(t[0] + t[1] + t[2] + t[3])
    first = iota2((LANES // 2, LANES), 1) < LANES // 2

    def increment(x, scaled):
        hi, lo = halves(scaled)
        both = folded(dot_tn(x, jnp.concatenate([hi, lo], axis=1)))
        return jnp.where(first, both[: LANES // 2], both[LANES // 2 :])

    refs["state"][:, at] = increment(refs["v"][:, at], refs["k"][:, at].astype(F32) * tail)
    refs["grad"][:, at] = increment(refs["dy"][:, at], refs["r"][:, at].astype(F32) * early)


def phase_two(i, refs):
    at = pl.ds(pl.multiple_of(i * LANES, LANES), LANES)
    r, k = refs["r"][:, at].astype(F32), refs["k"][:, at].astype(F32)
    v, dy = refs["v"][:, at], refs["dy"][:, at]
    upto, before = refs["upto"][:, at], refs["before"][:, at]
    tok = r.shape[0]
    t = totals_of(upto)
    zero = jnp.zeros_like(t[0])
    whole = rows_of(t)
    half = 0.5 * whole
    v_heads, dy_heads = per_head(v), per_head(dy)
    scores = halves(dot_nt(dy, v_heads))
    scores_t = halves(dot_nt(v, dy_heads))
    row = iota2((tok, 2 * tok), 0)
    col = iota2((tok, 2 * tok), 1) % tok
    early_1, tail_1 = jnp.exp(before), jnp.exp(whole - upto)
    levels = [
        (jnp.exp(before - half), jnp.exp(half - upto), lambda a, b: (b < a) & (a // BLOCK == b // BLOCK)),
        (
            early_1,
            tail_1,
            lambda a, b: (b // BLOCK < a // BLOCK) & (a // (2 * BLOCK) == b // (2 * BLOCK)),
        ),
        (
            early_1 * jnp.exp(rows_of([zero, zero, zero, t[2]])),
            tail_1 * jnp.exp(rows_of([t[1], zero, zero, zero])),
            lambda a, b: b // (2 * BLOCK) < a // (2 * BLOCK),
        ),
    ]
    rec = jnp.zeros((tok, LANES), F32)
    key = jnp.zeros((tok, LANES), F32)
    cross = jnp.zeros((tok, 2 * tok), F32)
    none = jnp.zeros((tok, 2 * tok), BF16)
    for r_scale, k_scale, inside in levels:
        lower, upper = inside(row, col), inside(col, row)
        r_heads = per_head_halves(r * r_scale)
        k_level = k * k_scale
        k_heads = per_head_halves(k_level)
        k_hi, k_lo = halves(k_level)
        rec_level = folded(dot_nn(jnp.where(lower, scores[0], none), k_heads))
        rec_level += dot_nn(jnp.where(lower, scores[1], none), k_heads[:, :LANES])
        rec += rec_level * r_scale
        key_level = folded(dot_nn(jnp.where(upper, scores_t[0], none), r_heads))
        key_level += dot_nn(jnp.where(upper, scores_t[1], none), r_heads[:, :LANES])
        key += key_level * k_scale
        cross_level = dot_nt(k_hi, r_heads[:, :LANES]) + (
            dot_nt(k_hi, r_heads[:, LANES:]) + dot_nt(k_lo, r_heads[:, :LANES])
        )
        cross += jnp.where(upper, cross_level, 0.0)
    cross_hi, cross_lo = halves(cross)
    val = dot_nn(cross_hi, dy_heads) + dot_nn(cross_lo, dy_heads)
    boost = refs["u"][:, at]
    same = (iota2((LANES, LANES), 0) < LANES // 2) == (iota2((LANES, LANES), 1) < LANES // 2)
    ones = jnp.where(same, 1.0, 0.0).astype(BF16)
    dy_f = dy.astype(F32)
    own_r, own_k = r * boost, k * boost
    vd_hi, vd_lo = halves(v.astype(F32) * dy_f)
    rk_hi, rk_lo = halves(own_r * k)
    scalar = dot_nn(vd_hi, ones) + dot_nn(vd_lo, ones)
    factor = dot_nn(rk_hi, ones) + dot_nn(rk_lo, ones)
    refs["rec"][:, at] = rec + own_k * scalar
    refs["key"][:, at] = key + own_r * scalar
    refs["val"][:, at] = val + factor * dy_f


def phase_three(i, refs):
    at = pl.ds(pl.multiple_of(i * LANES, LANES), LANES)
    v, dy = refs["v"][:, at], refs["dy"][:, at]
    early, tail = refs["early"][:, at], refs["tail"][:, at]
    state_in = per_head_halves(refs["state_in"][:, at])
    grad_in = per_head_halves(refs["grad_in"][:, at])
    grad_hi, grad_lo = grad_in[:, :LANES], grad_in[:, LANES:]
    k_hi, k_lo = halves(refs["k"][:, at].astype(F32) * tail)
    rec = refs["rec"][:, at] + early * folded(dot_nn(dy, state_in))
    key = refs["key"][:, at] + tail * folded(dot_nn(v, grad_in))
    val = refs["val"][:, at] + (dot_nt(k_hi, grad_hi) + (dot_nt(k_hi, grad_lo) + dot_nt(k_lo, grad_hi)))
    refs["rec_out"][:, at] = rec.astype(BF16)
    refs["key_out"][:, at] = key.astype(BF16)
    refs["val_out"][:, at] = val.astype(BF16)


ONE = ("r", "k", "v", "f", "u", "dy")
ONE_OUT = ("state", "grad", "decay", "rec", "key", "val", "early", "tail")


def kernel_one(pairs, *refs):
    named = dict(zip(ONE + ONE_OUT + ("upto", "before"), refs))
    lax.fori_loop(0, pairs, lambda i, c: (phase_one(i, named), c)[1], 0)
    lax.fori_loop(0, pairs, lambda i, c: (phase_two(i, named), c)[1], 0)


TWO = ("k", "v", "dy", "rec", "key", "val", "early", "tail", "state_in", "grad_in")


def kernel_two(pairs, *refs):
    named = dict(zip(TWO + ("rec_out", "key_out", "val_out"), refs))
    lax.fori_loop(0, pairs, lambda i, c: (phase_three(i, named), c)[1], 0)


def local_part(r, k, v, f, u, dy):
    tok, width = r.shape
    half = LANES // 2
    shapes = [(half, width)] * 2 + [(1, width)] + [(tok, width)] * 5
    return pl.pallas_call(
        functools.partial(kernel_one, width // LANES),
        out_shape=[jax.ShapeDtypeStruct(s, F32) for s in shapes],
        in_specs=[pl.BlockSpec(memory_space=pltpu.VMEM)] * 6,
        out_specs=[pl.BlockSpec(memory_space=pltpu.VMEM)] * 8,
        scratch_shapes=[pltpu.VMEM((tok, width), F32)] * 2,
        compiler_params=pltpu.CompilerParams(vmem_limit_bytes=48 << 20),
        cost_estimate=pl.CostEstimate(flops=1 << 31, bytes_accessed=8 << 20, transcendentals=0),
    )(r, k, v, f, u, dy)


def last_part(k, v, dy, rec, key, val, early, tail, state_in, grad_in):
    tok, width = k.shape
    return pl.pallas_call(
        functools.partial(kernel_two, width // LANES),
        out_shape=[jax.ShapeDtypeStruct((tok, width), BF16)] * 3,
        in_specs=[pl.BlockSpec(memory_space=pltpu.VMEM)] * 10,
        out_specs=[pl.BlockSpec(memory_space=pltpu.VMEM)] * 3,
        compiler_params=pltpu.CompilerParams(vmem_limit_bytes=48 << 20),
        cost_estimate=pl.CostEstimate(flops=1 << 29, bytes_accessed=8 << 20, transcendentals=0),
    )(k, v, dy, rec, key, val, early, tail, state_in, grad_in)


def carried(decay, value, start, axis, reverse):
    count, position = lax.axis_size(axis), lax.axis_index(axis)
    decay_all, value_all = lax.all_gather(decay, axis), lax.all_gather(value, axis)
    total, product = start, jnp.ones_like(decay)
    for n in range(count):
        at = count - 1 - n if reverse else n
        reached = at > position if reverse else at < position
        total = jnp.where(reached, decay_all[at] * total + value_all[at], total)
        product = jnp.where(reached, decay_all[at] * product, product)
    return product, total


def sent_and_summed(value, axis):
    arrived = lax.all_to_all(value, axis, split_axis=0, concat_axis=0, tiled=True)
    return arrived.sum(axis=0)


def on_device(r, k, v, f, u, dy, initial):
    batch, tok, width = r.shape
    heads, size = u.shape
    r, k, v, f, dy = (x.reshape(tok, width) for x in (r, k, v, f, dy))
    state, grad, decay, rec, key, val, early, tail = local_part(r, k, v, f, u.reshape(1, width), dy)
    prefix, state_in = carried(decay, state, initial.T, "seq", False)
    _, grad_in = carried(decay, grad, jnp.zeros_like(grad), "seq", True)
    outs = last_part(k, v, dy, rec, key, val, early, tail, state_in, grad_in)
    dp, seq = lax.axis_size("dp"), lax.axis_size("seq")
    term = (prefix * grad).reshape(size, dp, width // dp).transpose(1, 0, 2)
    summed = sent_and_summed(term.reshape(dp, size * width // dp // LANES, LANES), "dp")
    summed = sent_and_summed(summed.reshape(seq, size * width // dp // seq), "seq")
    state_grad = summed.reshape(size // seq, width // dp).T
    return tuple(x.reshape(batch, tok, width) for x in outs) + (state_grad,)


def solution(mesh):
    rows = P("dp", "seq", None)
    return jax.shard_map(
        on_device,
        mesh=mesh,
        in_specs=(rows, rows, rows, rows, P(), rows, P()),
        out_specs=(rows, rows, rows, P("dp", "seq")),
        check_vma=False,
    )
```

profile of v0, /device:TPU:1, one launch (start us, length us, event | category | flops | bytes accessed | tf_op | source)
XLA Modules:
  0.0 174.5 jit_solution(4152000307271273632)
XLA Ops:
  7.2 0.0 all-gather.7.cloned.1.call-start
  7.2 0.8 reshape.131.refs_4_
  8.0 0.0 copy-start.1
  8.0 1.0 copy-done.1
  9.1 0.0 copy-start.3
  9.1 1.0 copy-done.3
  10.1 0.0 copy-start.5
  10.1 1.0 copy-done.5
  11.1 0.0 copy-start.7
  11.1 1.0 copy-done.7
  12.2 0.0 copy-start.8
  12.2 1.0 copy-done.8
  13.2 22.3 %shard_map.102 = (f32[64,2048]{1,0:T(8,128)}, f32[64,2048]{1,0:T(8,128)}, f32[1,2048]{1,0:T(1,128)S(1)}, f32[128,2048]{1,0:T(8,128)S(1)}, f32[128,2048]{1,0:T(8,...) custom-call(bf16[128,2048]{1,0:T(8,128)(2,1)S(1)} %bitcast.37, ...), custom_call_target="tpu_custom_call" | custom-call | flops 2147483648 | bytes 8388608 | tf_op jit(solution)/shard_map/pallas_call | solution.py:204
  35.5 0.0 all-gather.7.cloned.1.call-update
  35.5 0.0 all-gather.9.cloned.1.call-start
  35.6 0.7 all-gather.9.cloned.1.call-update
  36.3 26.5 %all-gather.3 = f32[8,1,2048]{2,1,0:T(1,128)S(1)} all-gather(f32[1,1,2048]{2,1,0:T(1,128)S(1)} %bitcast.36), channel_id=2, replica_groups=mesh['seq'=8,'dp'=64] {'seq'}, dimensions={0}, use_global_device_ids=true | all-gather | bytes 73728 | tf_op jit(solution)/shard_map/all_gather | solution.py:229
  62.9 1.9 %broadcast_multiply_fusion = f32[64,2048]{1,0:T(8,128)} fusion(f32[64,2048]{1,0:T(8,128)} %get-tuple-element.22, f32[2048]{0:T(1024)S(1)} %get-tuple-element.34), kind=kLoop, calls=%fused_computation.33 | loop fusion | flops 131072 | bytes 1056768 | tf_op jit(solution)/shard_map/mul | solution.py:253
  64.8 1.4 copy.13
  66.1 2.0 %copy.14 = f32[64,64,32]{0,2,1:T(8,128)} copy(f32[64,64,32]{1,2,0:T(8,128)S(1)} %bitcast.39) | data formatting | bytes 1048576 | tf_op jit(solution)/shard_map/transpose | solution.py:253
  68.1 1.6 copy.15
  69.8 33.9 %all_to_all.14 = f32[64,16,128]{2,1,0:T(8,128)S(1)} all-to-all(f32[64,16,128]{2,1,0:T(8,128)S(1)} %copy.15), channel_id=1, replica_groups=mesh['seq'=8,'dp'=64] {'dp'}, dimensions={0} | all-to-all | bytes 1048576 | tf_op jit(solution)/shard_map/all_to_all | solution.py:240
  103.7 0.7 reduce_sum.18
  104.3 3.7 %all-to-all-start.1 = ((f32[8,1,256]{2,1,0:T(1,128)}), f32[8,1,256]{2,1,0:T(1,128)S(1)}, u32[]{:S(2)}, u32[]{:S(2)}) async-start(f32[8,1,256]{2,1,0:T(1,128)} %bitcast.21), calls=%async_computation.1 | async-start | bytes 16384 | tf_op jit(solution)/shard_map/all_to_all | solution.py:240
  108.0 6.6 %all-to-all-done.1 = f32[8,1,256]{2,1,0:T(1,128)S(1)} async-done(((f32[8,1,256]{2,1,0:T(1,128)}), f32[8,1,256]{2,1,0:T(1,128)S(1)}, u32[]{:S(2)}, u32[]{:S(2)}) %all-to-all-start.1) | async-done | bytes 8224 | tf_op jit(solution)/shard_map/all_to_all | solution.py:240
  114.6 0.7 reshape.137
  115.3 0.0 copy-start.2
  115.3 0.0 all-gather.7.cloned.1.call-done
  115.3 2.8 %fusion.8.refs_8_ = f32[64,2048]{1,0:T(8,128)S(1)} fusion(f32[512,2048]{1,0:T(8,128)} %all-gather.7.cloned.1.call-done, f32[2048,64]{0,1:T(8,128)} %param.13, f32[2048]{0:T(1024)S(1)} %bitcast.60, f32[2048]{0:T(1024)S(1)} %bitcast.42, f32[2048]{0:T(1024)S(1)} %bitcast.45, f32[2048]{0:T(1024)S(1)} %bitcast.48, f32[2048]{0:T(1024)S(1)} %bitcast.51, ...), kind=kLoop, calls=%fused_computation.17 | loop fusion | flops 3145728 | bytes 5308424 | tf_op jit(solution)/shard_map/jit(_where)/select_n | solution.py:234
  118.1 40.2 %all-gather.9.cloned.1.call-done = f32[512,2048]{1,0:T(8,128)} async-done(((f32[64,2048]{1,0:T(8,128)}), f32[512,2048]{1,0:T(8,128)}) %all-gather.9.cloned.1.call-update) | async-done | bytes 4194320 | tf_op jit(solution)/shard_map/all_gather | solution.py:229
  158.3 0.0 copy-start
  158.3 0.0 copy-start.4
  158.3 0.0 copy-start.6
  158.3 2.7 %fusion.refs_9_ = f32[64,2048]{1,0:T(8,128)S(1)} fusion(f32[512,2048]{1,0:T(8,128)} %all-gather.9.cloned.1.call-done, f32[2048]{0:T(1024)S(1)} %get-tuple-element.35, f32[2048]{0:T(1024)S(1)} %bitcast.61, f32[2048]{0:T(1024)S(1)} %bitcast.43, f32[2048]{0:T(1024)S(1)} %bitcast.46, f32[2048]{0:T(1024)S(1)} %bitcast.49, f32[2048]{0:T(1024)S(1)} %bitcast.52, ...), kind=kLoop, calls=%fused_computation.1 | loop fusion | flops 3014656 | bytes 4784136 | tf_op jit(solution)/shard_map/jit(_where)/select_n | solution.py:234
  161.0 0.0 copy-done.2
  161.1 0.0 copy-done
  161.1 0.0 copy-done.4
  161.1 0.0 copy-done.6
  161.1 6.5 %shard_map.103 = (bf16[128,2048]{1,0:T(8,128)(2,1)}, bf16[128,2048]{1,0:T(8,128)(2,1)}, bf16[128,2048]{1,0:T(8,128)(2,1)}) custom-call(bf16[128,2048]{1,0:T(8,128)(2,1)S(1)} %bitcast.31, bf16[128,2048]{1,0:T(8,128)(2,1)S(1)} %bitcast.33, bf16[128,2048]{1,0:T(8,128)(2,1)S(1)} %bitcast.35, f32[128,2048]{1,0:T(8,128)S(1)} %get-tuple-element.15.refs_3_, ...), custom_call_target="tpu_custom_call" | custom-call | flops 536870912 | bytes 8388608 | tf_op jit(solution)/shard_map/pallas_call | solution.py:217
  (3 shorter events, 0.1 us)
Async XLA Ops:
  7.2 108.1 %all-gather.7.cloned.1.call-start = ((), (), s32[]{:S(2)}) async-start(), calls=%async_computation.2 | async-start | bytes 4718592 | tf_op jit(solution)/shard_map/all_gather | solution.py:229
  8.0 1.0 copy-start.1
  9.1 1.0 copy-start.3
  10.1 1.0 copy-start.5
  11.1 1.0 copy-start.7
  12.2 1.0 copy-start.8
  35.5 122.8 %all-gather.9.cloned.1.call-start = ((), (), s32[]{:S(2)}) async-start(), calls=%async_computation.3 | async-start | bytes 4718592 | tf_op jit(solution)/shard_map/all_gather | solution.py:229
  104.3 10.3 %all-to-all-start.1 = ((f32[8,1,256]{2,1,0:T(1,128)}), f32[8,1,256]{2,1,0:T(1,128)S(1)}, u32[]{:S(2)}, u32[]{:S(2)}) async-start(f32[8,1,256]{2,1,0:T(1,128)} %bitcast.21), calls=%async_computation.1 | async-start | bytes 16384 | tf_op jit(solution)/shard_map/all_to_all | solution.py:240
  115.3 45.8 %copy-start.2 = (bf16[1,128,2048]{2,1,0:T(8,128)(2,1)S(1)}, bf16[1,128,2048]{2,1,0:T(8,128)(2,1)}, u32[]{:S(2)}) copy-start(bf16[1,128,2048]{2,1,0:T(8,128)(2,1)} %param.8) | copy-start | bytes 1572868
  158.3 2.7 %copy-start = (f32[128,2048]{1,0:T(8,128)S(1)}, f32[128,2048]{1,0:T(8,128)}, u32[]{:S(2)}) copy-start(f32[128,2048]{1,0:T(8,128)} %get-tuple-element.17.refs_5_) | copy-start | bytes 3145732
  158.3 2.7 %copy-start.4 = (bf16[1,128,2048]{2,1,0:T(8,128)(2,1)S(1)}, bf16[1,128,2048]{2,1,0:T(8,128)(2,1)}, u32[]{:S(2)}) copy-start(bf16[1,128,2048]{2,1,0:T(8,128)(2,1)} %param.9) | copy-start | bytes 1572868
  158.3 2.8 %copy-start.6 = (bf16[1,128,2048]{2,1,0:T(8,128)(2,1)S(1)}, bf16[1,128,2048]{2,1,0:T(8,128)(2,1)}, u32[]{:S(2)}) copy-start(bf16[1,128,2048]{2,1,0:T(8,128)(2,1)} %param.12) | copy-start | bytes 1572868
Sparse Core Ops, SparseCore 0:
  35.7 63.7 all-gather.6
  102.2 56.1 all-gather.8
where the time goes:
time: 175 us; the launch traced here: 174 us
  blocking collectives  60.4 us (35%)
  waiting for transfers between devices  47.5 us (27%)
  Pallas kernels  28.8 us (16%)
  between operations  14.1 us (8%)
  local copies, waits for them, and re-layouts  11.7 us (7%)
  other arithmetic  8.15 us (5%)
  starting transfers between devices  3.77 us (2%)
    all_gather x2, waiting for transfers between devices, carried(): lax.all_gather(value, axis)  40.2 us
    all_to_all x1, blocking collectives, sent_and_summed(): lax.all_to_all(value, axis, split_axis=0, concat_axis=0, tiled=True)  33.9 us
    all_gather x1, blocking collectives, carried(): lax.all_gather(decay, axis)  26.5 us
    pallas_call x1, Pallas kernels, local_part(): pl.pallas_call(functools.partial(kernel_one, width // LANES), out_shape=[...  22.3 us
    all_to_all x1, waiting for transfers between devices, sent_and_summed(): lax.all_to_all(value, axis, split_axis=0, concat_axis=0, tiled=True)  6.58 us
    pallas_call x1, Pallas kernels, last_part(): pl.pallas_call(functools.partial(kernel_two, width // LANES), out_shape=[...  6.54 us
    select_n x2, other arithmetic, carried(): total = jnp.where(reached, decay_all[at] * total + value_all[at], total)  5.55 us
    unnamed x18, local copies, waits for them, and re-layouts  5.23 us
  transfers between devices with their start and end apart: 3, of which 2 were waited for; matrix products, arithmetic and copies ran while one was open for 6% of the time, Pallas kernels for 0%

commit v1 on v0

v1 whole, which is shorter than its diff:
```python
import functools

import jax
import jax.numpy as jnp
from jax import lax
from jax.experimental import pallas as pl
from jax.experimental.pallas import tpu as pltpu
from jax.sharding import PartitionSpec as P

F32 = jnp.float32
BF16 = jnp.bfloat16
LANES = 128
BLOCK = 32


def dot_nn(a, b):
    return lax.dot_general(a, b, (((1,), (0,)), ((), ())), preferred_element_type=F32)


def dot_nt(a, b):
    return lax.dot_general(a, b, (((1,), (1,)), ((), ())), preferred_element_type=F32)


def dot_tn(a, b):
    return lax.dot_general(a, b, (((0,), (0,)), ((), ())), preferred_element_type=F32)


def halves(x):
    hi = x.astype(BF16)
    return hi, (x - hi.astype(F32)).astype(BF16)


def thirds(x):
    hi = x.astype(BF16)
    rest = x - hi.astype(F32)
    mid = rest.astype(BF16)
    return hi, mid, (rest - mid.astype(F32)).astype(BF16)


def iota2(shape, dim):
    return lax.broadcasted_iota(jnp.int32, shape, dim)


def per_head(x):
    first = iota2(x.shape, 1) < LANES // 2
    zero = jnp.zeros_like(x)
    return jnp.concatenate([jnp.where(first, x, zero), jnp.where(first, zero, x)], axis=0)


def per_head_halves(x):
    hi, lo = halves(per_head(x))
    return jnp.concatenate([hi, lo], axis=1)


def folded(x):
    return x[:, :LANES] + x[:, LANES:]


def rows_of(parts):
    return jnp.concatenate([jnp.broadcast_to(p, (BLOCK, LANES)) for p in parts], axis=0)


def decays(f_ref, at):
    tok = f_ref.shape[0]
    log_w = -jnp.exp(f_ref[:, at].astype(F32))
    row, col = iota2((tok, tok), 0), iota2((tok, tok), 1)
    tri = jnp.where((col <= row) & (col // BLOCK == row // BLOCK), 1.0, 0.0).astype(BF16)
    hi, mid, lo = thirds(log_w)
    sums = dot_nn(tri, jnp.concatenate([hi, mid, lo], axis=1))
    upto = sums[:, :LANES] + (sums[:, LANES : 2 * LANES] + sums[:, 2 * LANES :])
    return upto, upto - log_w


def totals_of(upto):
    return [upto[b * BLOCK + BLOCK - 1 : (b + 1) * BLOCK] for b in range(upto.shape[0] // BLOCK)]


def shard_sums(upto):
    t = totals_of(upto)
    zero = jnp.zeros_like(t[0])
    ahead = [zero, t[0], t[0] + t[1], t[0] + t[1] + t[2]]
    behind = [t[1] + t[2] + t[3], t[2] + t[3], t[3], zero]
    return t, ahead, behind, t[0] + behind[0]


def lanes_at(i):
    return pl.ds(pl.multiple_of(i * LANES, LANES), LANES)


def phase_one(i, refs):
    at = lanes_at(i)
    upto, before = decays(refs["f"], at)
    t, ahead, behind, everything = shard_sums(upto)
    early = jnp.exp(before + rows_of(ahead))
    tail = jnp.exp(rows_of([a + b for a, b in zip(t, behind)]) - upto)
    refs["upto"][:, at] = upto
    refs["before"][:, at] = before
    refs["early"][:, at] = early
    refs["tail"][:, at] = tail
    refs["decay"][pl.ds(i, 1), :] = jnp.exp(everything)
    first = iota2((LANES // 2, LANES), 1) < LANES // 2

    def increment(x, scaled):
        hi, lo = halves(scaled)
        both = folded(dot_tn(x, jnp.concatenate([hi, lo], axis=1)))
        return jnp.where(first, both[: LANES // 2], both[LANES // 2 :])

    refs["state"][i] = increment(refs["v"][:, at], refs["k"][:, at].astype(F32) * tail)
    refs["grad"][i] = increment(refs["dy"][:, at], refs["r"][:, at].astype(F32) * early)


def phase_two(i, refs):
    at = lanes_at(i)
    r, k = refs["r"][:, at].astype(F32), refs["k"][:, at].astype(F32)
    v, dy = refs["v"][:, at], refs["dy"][:, at]
    upto, before = refs["upto"][:, at], refs["before"][:, at]
    tok = r.shape[0]
    t = totals_of(upto)
    zero = jnp.zeros_like(t[0])
    whole = rows_of(t)
    half = 0.5 * whole
    v_heads, dy_heads = per_head(v), per_head(dy)
    scores = halves(dot_nt(dy, v_heads))
    scores_t = halves(dot_nt(v, dy_heads))
    row = iota2((tok, 2 * tok), 0)
    col = iota2((tok, 2 * tok), 1) % tok
    early_1, tail_1 = jnp.exp(before), jnp.exp(whole - upto)
    levels = [
        (jnp.exp(before - half), jnp.exp(half - upto), lambda a, b: (b < a) & (a // BLOCK == b // BLOCK)),
        (
            early_1,
            tail_1,
            lambda a, b: (b // BLOCK < a // BLOCK) & (a // (2 * BLOCK) == b // (2 * BLOCK)),
        ),
        (
            early_1 * jnp.exp(rows_of([zero, zero, zero, t[2]])),
            tail_1 * jnp.exp(rows_of([t[1], zero, zero, zero])),
            lambda a, b: b // (2 * BLOCK) < a // (2 * BLOCK),
        ),
    ]
    rec = jnp.zeros((tok, LANES), F32)
    key = jnp.zeros((tok, LANES), F32)
    cross = jnp.zeros((tok, 2 * tok), F32)
    none = jnp.zeros((tok, 2 * tok), BF16)
    for r_scale, k_scale, inside in levels:
        lower, upper = inside(row, col), inside(col, row)
        r_heads = per_head_halves(r * r_scale)
        k_level = k * k_scale
        k_heads = per_head_halves(k_level)
        k_hi, k_lo = halves(k_level)
        rec_level = folded(dot_nn(jnp.where(lower, scores[0], none), k_heads))
        rec_level += dot_nn(jnp.where(lower, scores[1], none), k_heads[:, :LANES])
        rec += rec_level * r_scale
        key_level = folded(dot_nn(jnp.where(upper, scores_t[0], none), r_heads))
        key_level += dot_nn(jnp.where(upper, scores_t[1], none), r_heads[:, :LANES])
        key += key_level * k_scale
        cross_level = dot_nt(k_hi, r_heads[:, :LANES]) + (
            dot_nt(k_hi, r_heads[:, LANES:]) + dot_nt(k_lo, r_heads[:, :LANES])
        )
        cross += jnp.where(upper, cross_level, 0.0)
    cross_hi, cross_lo = halves(cross)
    val = dot_nn(cross_hi, dy_heads) + dot_nn(cross_lo, dy_heads)
    boost = jnp.concatenate([refs["u"][pl.ds(2 * i, 1), :], refs["u"][pl.ds(2 * i + 1, 1), :]], axis=1)
    same = (iota2((LANES, LANES), 0) < LANES // 2) == (iota2((LANES, LANES), 1) < LANES // 2)
    ones = jnp.where(same, 1.0, 0.0).astype(BF16)
    dy_f = dy.astype(F32)
    own_r, own_k = r * boost, k * boost
    vd_hi, vd_lo = halves(v.astype(F32) * dy_f)
    rk_hi, rk_lo = halves(own_r * k)
    scalar = dot_nn(vd_hi, ones) + dot_nn(vd_lo, ones)
    factor = dot_nn(rk_hi, ones) + dot_nn(rk_lo, ones)
    refs["rec"][:, at] = rec + own_k * scalar
    refs["key"][:, at] = key + own_r * scalar
    refs["val"][:, at] = val + factor * dy_f


def phase_three(i, refs):
    at = lanes_at(i)
    v, dy = refs["v"][:, at], refs["dy"][:, at]
    early, tail = refs["early"][:, at], refs["tail"][:, at]
    state_in = per_head_halves(refs["state_in"][i])
    grad_in = per_head_halves(refs["grad_in"][i])
    grad_hi, grad_lo = grad_in[:, :LANES], grad_in[:, LANES:]
    k_hi, k_lo = halves(refs["k"][:, at].astype(F32) * tail)
    rec = refs["rec"][:, at] + early * folded(dot_nn(dy, state_in))
    key = refs["key"][:, at] + tail * folded(dot_nn(v, grad_in))
    val = refs["val"][:, at] + (dot_nt(k_hi, grad_hi) + (dot_nt(k_hi, grad_lo) + dot_nt(k_lo, grad_hi)))
    refs["rec_done"][:, at] = rec.astype(BF16)
    refs["key_done"][:, at] = key.astype(BF16)
    refs["val_done"][:, at] = val.astype(BF16)


X_SIZE = 4
HOP = 3
TERM_AT, CORE_AT, X_AT, Y_AT, Z_AT, LAST_AT = 5, 7, 13, 19, 26, 30

OUT = ("rec_out", "key_out", "val_out", "state_grad")


def kernel(seq_size, dp_size, names, *all_refs):
    g = dict(zip(names, all_refs))
    pairs = g["state"].shape[0]
    half = LANES // 2
    x_size, y_size = X_SIZE, dp_size // (2 * X_SIZE)
    z, d = lax.axis_index("seq"), lax.axis_index("dp")
    c = d % 2
    x = (d // 2) % x_size
    y = d // (2 * x_size)
    last = seq_size - 1

    def chip(x_at, y_at, c_at):
        return {"dp": (y_at * x_size + x_at) * 2 + c_at}

    barrier = pltpu.get_barrier_semaphore()
    peers = [{"seq": (z + n) % seq_size} for n in range(1, seq_size)]
    peers += [chip((x + n) % x_size, y, c) for n in range(1, x_size)]
    peers += [chip(x, (y + n) % y_size, c) for n in range(1, y_size)]
    peers += [chip(x, y, 1 - c)]
    for peer in peers:
        pl.semaphore_signal(barrier, inc=1, device_id=peer, device_id_type=pl.DeviceIdType.MESH)

    loads = [
        pltpu.make_async_copy(g[n + "_hbm"], g[n], g["load_sem"].at[at]) for at, n in enumerate(("f", "k", "v", "r", "dy"))
    ]
    for load in loads:
        load.start()
    load_initial = pltpu.make_async_copy(g["initial_hbm"], g["initial"], g["load_sem"].at[5])

    @pl.when(z == 0)
    def _():
        load_initial.start()

    def remote(src, dst, send, recv, to):
        return pltpu.make_async_remote_copy(
            src_ref=src, dst_ref=dst, send_sem=send, recv_sem=recv, device_id=to, device_id_type=pl.DeviceIdType.MESH
        )

    def forward(j):
        to = {"seq": (z + 1) % seq_size}
        return remote(g["state_out"].at[j], g["state_in"].at[j], g["fs"].at[j], g["fr"].at[j], to)

    def backward(j):
        to = {"seq": (z + last) % seq_size}
        return remote(g["grad_out"].at[j], g["grad_in"].at[j], g["bs"].at[j], g["br"].at[j], to)

    def forward_on(j):
        g["state_out"][j] = g["decay"][pl.ds(j, 1), :] * g["state_in"][j] + g["state"][j]
        forward(j).start()

    def backward_on(j):
        g["grad_out"][j] = g["decay"][pl.ds(j, 1), :] * g["grad_in"][j] + g["grad"][j]
        backward(j).start()

    for load in loads:
        load.wait()

    @pl.when(z == 0)
    def _():
        load_initial.wait()

    pl.semaphore_wait(barrier, len(peers))

    def start_step(i, carry):
        phase_one(i, g)

        @pl.when(z == 0)
        def _():
            g["state_in"][i] = g["initial"][:, lanes_at(i)]
            forward_on(i)

        @pl.when(z == last)
        def _():
            g["grad_in"][i] = jnp.zeros((half, LANES), F32)
            backward_on(i)

        return carry

    lax.fori_loop(0, pairs, start_step, 0)

    def decay_to(n):
        return remote(g["decay"], g["decays"].at[z], g["ds"].at[n - 1], g["dr"].at[z], {"seq": (z + n) % seq_size})

    for n in range(1, seq_size):

        @pl.when(z + n <= last)
        def _():
            decay_to(n).start()

    def core_copy():
        return remote(
            g["term"].at[:, :, pl.ds(pl.multiple_of(16 * (1 - c), 16), 16)],
            g["core_in"],
            g["cs"].at[0],
            g["cr"].at[0],
            chip(x, y, 1 - c),
        )

    def x_copy(n):
        to = (x + n) % x_size
        return remote(g["summed"].at[:, to], g["x_in"].at[n - 1], g["xs"].at[n - 1], g["xr"].at[n - 1], chip(to, y, c))

    def y_copy(n):
        to = (y + n) % y_size
        return remote(g["x_sum"].at[to], g["y_in"].at[n - 1], g["ys"].at[n - 1], g["yr"].at[n - 1], chip(x, to, c))

    def z_copy(n):
        b, hi = n % 2, n // 2
        to = 2 * c + b + 4 * hi
        return to, remote(g["y_sum"].at[pl.ds(8 * b, 8)], g["z_in"].at[z], g["zs"].at[n], g["zr"].at[z], {"seq": to})

    def last_copy():
        return remote(g["z_sum"], g["z_other"], g["cs"].at[1], g["cr"].at[1], chip(x, y, 1 - c))

    gathers = (z % 4) // 2 == c

    def make_terms():
        g["prefix"][...] = jnp.ones((pairs, LANES), F32)
        for q in range(last):

            @pl.when(q < z)
            def _():
                remote(g["decay"], g["decays"].at[q], g["ds"].at[0], g["dr"].at[q], {"seq": z}).wait_recv()
                g["prefix"][...] = g["prefix"][...] * g["decays"][q]

        first = iota2((half // 2, LANES), 1) < half

        def one(i, carry):
            t = g["prefix"][pl.ds(i, 1), :] * g["grad"][i]
            top, low = t[: half // 2], t[half // 2 :]
            h = 2 * i
            g["term"][h // x_size, h % x_size] = jnp.where(first, top, pltpu.roll(low, half, 1))
            g["term"][h // x_size, h % x_size + 1] = jnp.where(first, pltpu.roll(top, half, 1), low)
            return carry

        lax.fori_loop(0, pairs, one, 0)
        core_copy().start()

    def sum_core():
        core_copy().wait_recv()

        def one(n, carry):
            own = g["term"][n // x_size, n % x_size, pl.ds(pl.multiple_of(16 * c, 16), 16)]
            g["summed"][n // x_size, n % x_size] = own + g["core_in"][n // x_size, n % x_size]
            return carry

        lax.fori_loop(0, x_size * y_size, one, 0)
        for n in range(1, x_size):
            x_copy(n).start()

    def sum_x():
        for n in range(1, x_size):
            x_copy(n).wait_recv()
        for at in range(y_size):
            total = g["summed"][at, x]
            for n in range(1, x_size):
                total += g["x_in"][n - 1, at]
            g["x_sum"][at] = total
        for n in range(1, y_size):
            y_copy(n).start()

    def sum_y():
        for n in range(1, y_size):
            y_copy(n).wait_recv()
        total = g["x_sum"][y]
        for n in range(1, y_size):
            total += g["y_in"][n - 1]
        g["y_sum"][...] = total
        for n in range(4):
            to, copy = z_copy(n)

            @pl.when(to != z)
            def _():
                copy.start()

            @pl.when(to == z)
            def _():
                g["z_in"][z] = g["y_sum"][pl.ds(8 * (n % 2), 8)]

    def sum_z():
        @pl.when(gathers)
        def _():
            for q in range(seq_size):

                @pl.when(z != q)
                def _():
                    remote(
                        g["y_sum"].at[pl.ds(0, 8)], g["z_in"].at[q], g["zs"].at[0], g["zr"].at[q], {"seq": q}
                    ).wait_recv()

            total = g["z_in"][0]
            for q in range(1, seq_size):
                total += g["z_in"][q]
            g["z_sum"][...] = total
            last_copy().start()

    def finish():
        @pl.when(jnp.logical_not(gathers))
        def _():
            last_copy().wait_recv()
            g["z_sum"][...] = g["z_other"][...]

        total = g["z_sum"][...]
        total = jnp.where(z // 4 == 1, pltpu.roll(total, half, 1), total)
        total = jnp.where(c == 1, pltpu.roll(total, LANES - half // 2, 1), total)
        g["state_grad"][...] = total[:, : half // 2]

    stages = ((TERM_AT, make_terms), (CORE_AT, sum_core), (X_AT, sum_x), (Y_AT, sum_y), (Z_AT, sum_z), (LAST_AT, finish))
    finals = ("rec", "key", "val")

    def store(n, j):
        at = lanes_at(j)
        name = finals[n]
        return pltpu.make_async_copy(g[name + "_done"].at[:, at], g[name + "_out"].at[:, at], g["store_sem"].at[n, j])

    def tick(n, carry):
        jf = n - HOP * z
        jb = n - HOP * (last - z)
        j = n - HOP * jnp.maximum(z, last - z)

        @pl.when((z > 0) & (jf >= 0) & (jf < pairs))
        def _():
            forward(jf).wait_recv()

            @pl.when(z < last)
            def _():
                forward_on(jf)

        @pl.when((z < last) & (jb >= 0) & (jb < pairs))
        def _():
            backward(jb).wait_recv()

            @pl.when(z > 0)
            def _():
                backward_on(jb)

        @pl.when(n < pairs)
        def _():
            phase_two(n, g)

        for at, stage in stages:
            pl.when(n == at)(stage)

        @pl.when((j >= 0) & (j < pairs))
        def _():
            phase_three(j, g)
            for m in range(3):
                store(m, j).start()

        return carry

    lax.fori_loop(0, HOP * last + pairs, tick, 0)

    @pl.when(z < last)
    def _():
        lax.fori_loop(0, pairs, lambda j, s: (forward(j).wait_send(), s)[1], 0)

    @pl.when(z > 0)
    def _():
        lax.fori_loop(0, pairs, lambda j, s: (backward(j).wait_send(), s)[1], 0)

    for n in range(1, seq_size):

        @pl.when(z + n <= last)
        def _():
            decay_to(n).wait_send()

    core_copy().wait_send()
    for n in range(1, x_size):
        x_copy(n).wait_send()
    for n in range(1, y_size):
        y_copy(n).wait_send()
    for n in range(4):
        to, copy = z_copy(n)

        @pl.when(to != z)
        def _():
            copy.wait_send()

    @pl.when(gathers)
    def _():
        last_copy().wait_send()

    for m in range(3):
        lax.fori_loop(0, pairs, lambda j, s: (store(m, j).wait(), s)[1], 0)


def on_device(seq_size, dp_size, r, k, v, f, u, dy, initial):
    batch, tok, width = r.shape
    heads, size = u.shape
    pairs, half = width // LANES, LANES // 2
    x_size, y_size = X_SIZE, dp_size // (2 * X_SIZE)
    dma = lambda *n: pltpu.SemaphoreType.DMA(n)
    vmem = lambda *s: pltpu.VMEM(s, F32)
    scratch = {n: pltpu.VMEM((tok, width), BF16) for n in ("r", "k", "v", "f", "dy", "rec_done", "key_done", "val_done")}
    scratch |= {n: vmem(tok, width) for n in ("upto", "before", "early", "tail", "rec", "key", "val")}
    scratch |= {n: vmem(pairs, half, LANES) for n in ("state", "grad", "state_in", "grad_in", "state_out", "grad_out")}
    scratch |= {
        "initial": vmem(size, width),
        "decay": vmem(pairs, LANES),
        "prefix": vmem(pairs, LANES),
        "decays": vmem(seq_size, pairs, LANES),
        "term": vmem(y_size, x_size, half // 2, LANES),
        "core_in": vmem(y_size, x_size, half // 4, LANES),
        "summed": vmem(y_size, x_size, half // 4, LANES),
        "x_in": vmem(x_size - 1, y_size, half // 4, LANES),
        "x_sum": vmem(y_size, half // 4, LANES),
        "y_in": vmem(max(y_size - 1, 1), half // 4, LANES),
        "y_sum": vmem(half // 4, LANES),
        "z_in": vmem(seq_size, 8, LANES),
        "z_sum": vmem(8, LANES),
        "z_other": vmem(8, LANES),
        "load_sem": dma(6),
        "store_sem": dma(3, pairs),
        "fs": dma(pairs),
        "fr": dma(pairs),
        "bs": dma(pairs),
        "br": dma(pairs),
        "ds": dma(seq_size),
        "dr": dma(seq_size),
        "cs": dma(2),
        "cr": dma(2),
        "xs": dma(x_size),
        "xr": dma(x_size),
        "ys": dma(y_size),
        "yr": dma(y_size),
        "zs": dma(4),
        "zr": dma(seq_size),
    }
    names = ("r_hbm", "k_hbm", "v_hbm", "f_hbm", "dy_hbm", "u", "initial_hbm") + OUT + tuple(scratch)
    anywhere = pl.BlockSpec(memory_space=pl.ANY)
    inside = pl.BlockSpec(memory_space=pltpu.VMEM)
    tokens = jax.ShapeDtypeStruct((tok, width), BF16)
    outs = pl.pallas_call(
        functools.partial(kernel, seq_size, dp_size, names),
        out_shape=[tokens] * 3 + [jax.ShapeDtypeStruct((size // seq_size, half // 2), F32)],
        in_specs=[anywhere] * 5 + [inside, anywhere],
        out_specs=[anywhere] * 3 + [inside],
        scratch_shapes=list(scratch.values()),
        compiler_params=pltpu.CompilerParams(vmem_limit_bytes=56 << 20, collective_id=0, has_side_effects=True),
    )(*(a.reshape(tok, width) for a in (r, k, v, f, dy)), u, initial.T)
    return tuple(o.reshape(batch, tok, width) for o in outs[:3]) + (outs[3].T,)


def solution(mesh):
    rows = P("dp", "seq", None)
    return jax.shard_map(
        functools.partial(on_device, mesh.shape["seq"], mesh.shape["dp"]),
        mesh=mesh,
        in_specs=(rows, rows, rows, rows, P(), rows, P()),
        out_specs=(rows, rows, rows, P("dp", "seq")),
        check_vma=False,
    )
```

time: 175 us -> 70.2 us (0.40)
  the two profiles are of different devices: /device:TPU:1 before, /device:TPU:2 now
where the time goes in v1:
time: 70.2 us; the launch traced here: 70 us
  Pallas kernels  64.8 us (92%)
  local copies, waits for them, and re-layouts  4.56 us (6%)
    pallas_call x1, Pallas kernels, on_device(): pl.pallas_call(functools.partial(kernel, seq_size, dp_size, names), out_s...  64.8 us
    unnamed x10, local copies, waits for them, and re-layouts  4.56 us

profile of v1, /device:TPU:2, one launch (start us, length us, event | category | flops | bytes accessed | tf_op | source)
XLA Modules:
  0.0 70.0 jit_solution(12539972523012114297)
XLA Ops:
  0.6 64.8 %shard_map.102 = (bf16[128,2048]{1,0:T(8,128)(2,1)}, bf16[128,2048]{1,0:T(8,128)(2,1)}, bf16[128,2048]{1,0:T(8,128)(2,1)}, f32[8,32]{1,0:T(8,128)}) custom-call(bf16[128,2048]{1,0:T(8,128)(2,1)} %bitcast.13, bf16[128,2048]{1,0:T(8,128)(2,1)} %bitcast.14, bf16[128,2048]{1,0:T(8,128)(2,1)} %bitcast.15, bf16[128,2048]{1,0:T(8,128)(2,1)} %bitcast.16, ...), custom_call_target="tpu_custom_call" | custom-call | tf_op jit(solution)/shard_map/pallas_call | solution.py:533
  65.4 0.0 copy-start.1
  65.4 1.9 %copy.15 = bf16[1,128,2048]{2,1,0:T(8,128)(2,1)} copy(bf16[1,128,2048]{2,1,0:T(8,128)(2,1)} %bitcast.12) | data formatting | bytes 1048576
  67.4 0.0 copy-done.1
  67.4 0.0 copy-start
  67.4 0.8 %copy.16 = bf16[1,128,2048]{2,1,0:T(8,128)(2,1)} copy(bf16[1,128,2048]{2,1,0:T(8,128)(2,1)S(1)} %bitcast.11) | data formatting | bytes 1048576
  68.2 0.4 copy-done
  68.6 0.0 copy-start.2
  68.6 0.8 %copy.17 = bf16[1,128,2048]{2,1,0:T(8,128)(2,1)} copy(bf16[1,128,2048]{2,1,0:T(8,128)(2,1)S(1)} %bitcast.10) | data formatting | bytes 1048576
  69.4 0.0 copy-done.2
  69.4 0.6 copy.18
Async XLA Ops:
  65.4 2.0 %copy-start.1 = (bf16[128,2048]{1,0:T(8,128)(2,1)S(1)}, bf16[128,2048]{1,0:T(8,128)(2,1)}, u32[]{:S(2)}) copy-start(bf16[128,2048]{1,0:T(8,128)(2,1)} %get-tuple-element.9) | copy-start | bytes 1572868
  67.4 1.2 %copy-start = (bf16[128,2048]{1,0:T(8,128)(2,1)S(1)}, bf16[128,2048]{1,0:T(8,128)(2,1)}, u32[]{:S(2)}) copy-start(bf16[128,2048]{1,0:T(8,128)(2,1)} %get-tuple-element.10) | copy-start | bytes 1572868
  68.6 0.8 %copy-start.2 = (f32[8,32]{1,0:T(8,128)S(1)}, f32[8,32]{1,0:T(8,128)}, u32[]{:S(2)}) copy-start(f32[8,32]{1,0:T(8,128)} %get-tuple-element.11) | copy-start | bytes 3076

commit v2 on v1

v2 whole, which is shorter than its diff:
```python
import functools
from types import SimpleNamespace

import jax
import jax.numpy as jnp
from jax import lax
from jax.experimental import pallas as pl
from jax.experimental.pallas import tpu as pltpu
from jax.sharding import PartitionSpec as P

F32 = jnp.float32
BF16 = jnp.bfloat16
LANES = 128
BLOCK = 32


def dot_nn(a, b):
    return lax.dot_general(a, b, (((1,), (0,)), ((), ())), preferred_element_type=F32)


def dot_nt(a, b):
    return lax.dot_general(a, b, (((1,), (1,)), ((), ())), preferred_element_type=F32)


def dot_tn(a, b):
    return lax.dot_general(a, b, (((0,), (0,)), ((), ())), preferred_element_type=F32)


def halves(x):
    hi = x.astype(BF16)
    return hi, (x - hi.astype(F32)).astype(BF16)


def thirds(x):
    hi = x.astype(BF16)
    rest = x - hi.astype(F32)
    mid = rest.astype(BF16)
    return hi, mid, (rest - mid.astype(F32)).astype(BF16)


def iota2(shape, dim):
    return lax.broadcasted_iota(jnp.int32, shape, dim)


def per_head_halves(x, heads):
    hi, lo = halves(x)
    return jnp.concatenate(
        [
            jnp.concatenate([hi * heads[0], lo * heads[0]], axis=1),
            jnp.concatenate([hi * heads[1], lo * heads[1]], axis=1),
        ],
        axis=0,
    )


def per_head_rows(x, heads):
    return jnp.concatenate([x * heads[0], x * heads[1]], axis=0)


def folded(x):
    return x[:, :LANES] + x[:, LANES:]


def rows_of(parts):
    return jnp.concatenate([jnp.broadcast_to(p, (BLOCK, LANES)) for p in parts], axis=0)


def decay_sums(f_pair, tri):
    log_w = -jnp.exp(f_pair.astype(F32))
    hi, mid, lo = thirds(log_w)
    sums = dot_nn(tri, jnp.concatenate([hi, mid, lo], axis=1))
    upto = sums[:, :LANES] + (sums[:, LANES : 2 * LANES] + sums[:, 2 * LANES :])
    return upto, upto - log_w


def totals_of(upto):
    return [upto[b * BLOCK + BLOCK - 1 : (b + 1) * BLOCK] for b in range(upto.shape[0] // BLOCK)]


def shard_sums(upto):
    t = totals_of(upto)
    zero = jnp.zeros_like(t[0])
    ahead = [zero, t[0], t[0] + t[1], t[0] + t[1] + t[2]]
    behind = [t[1] + t[2] + t[3], t[2] + t[3], t[3], zero]
    return t, ahead, behind


def lanes_at(i):
    return pl.ds(pl.multiple_of(i * LANES, LANES), LANES)


def rows_at(i, count):
    return pl.ds(pl.multiple_of(i * count, count), count)


def prepare(refs):
    tok = refs.tri.shape[0]
    row, col = iota2((tok, tok), 0), iota2((tok, tok), 1)
    same = row // BLOCK == col // BLOCK
    refs.tri[...] = jnp.where((col <= row) & same, 1.0, 0.0).astype(BF16)
    row, col = iota2((tok, 2 * tok), 0), iota2((tok, 2 * tok), 1) % tok
    same = row // BLOCK == col // BLOCK
    refs.lower[...] = jnp.where((col < row) & same, 1.0, 0.0).astype(BF16)
    upper = jnp.where((col > row) & same, 1.0, 0.0)
    refs.upper[...] = upper.astype(BF16)
    refs.upper_f[...] = upper
    row, col = iota2((tok // 2, 2 * tok), 0), iota2((tok // 2, 2 * tok), 1) % tok
    later, earlier = 2 * (row // BLOCK) + 1, 2 * (row // BLOCK)
    refs.lower_1[...] = jnp.where(col // BLOCK == later - 1, 1.0, 0.0).astype(BF16)
    upper = jnp.where(col // BLOCK == earlier + 1, 1.0, 0.0)
    refs.upper_1[...] = upper.astype(BF16)
    refs.upper_1f[...] = upper
    first = iota2((tok, LANES), 1) < LANES // 2
    refs.heads[0] = jnp.where(first, 1.0, 0.0).astype(BF16)
    refs.heads[1] = jnp.where(first, 0.0, 1.0).astype(BF16)
    same = (iota2((2 * LANES, LANES), 0) % LANES < LANES // 2) == (iota2((2 * LANES, LANES), 1) < LANES // 2)
    refs.ones[...] = jnp.where(same, 1.0, 0.0).astype(BF16)


def shard_decay(i, refs):
    rates = jnp.exp(refs.f[:, lanes_at(i)].astype(F32))
    refs.decay[pl.ds(i, 1), :] = jnp.exp(-jnp.sum(rates, axis=0, keepdims=True))


def phase_one(pairs, refs):
    first = iota2((LANES // 2, LANES), 1) < LANES // 2
    tri = refs.tri[...]
    done = []
    for i in pairs:
        at = lanes_at(i)
        upto, before = decay_sums(refs.f[:, at], tri)
        t, ahead, behind = shard_sums(upto)
        early = jnp.exp(before + rows_of(ahead))
        tail = jnp.exp(rows_of([a + b for a, b in zip(t, behind)]) - upto)

        def increment(x, scaled):
            hi, lo = halves(scaled)
            both = folded(dot_tn(x, jnp.concatenate([hi, lo], axis=1)))
            return jnp.where(first, both[: LANES // 2], both[LANES // 2 :])

        state = increment(refs.v[:, at], refs.k[:, at].astype(F32) * tail)
        grad = increment(refs.dy[:, at], refs.r[:, at].astype(F32) * early)
        done.append((i, at, upto, before, early, tail, state, grad))
    for i, at, upto, before, early, tail, state, grad in done:
        refs.upto[:, at] = upto
        refs.before[:, at] = before
        refs.early[:, at] = early
        refs.tail[:, at] = tail
        refs.state[i] = state
        refs.grad[i] = grad


def picked(x, blocks):
    return jnp.concatenate([x[b * BLOCK : (b + 1) * BLOCK] for b in blocks], axis=0)


def spread(parts, values, blocks):
    for n, b in enumerate(blocks):
        parts[b] = parts[b] + values[n * BLOCK : (n + 1) * BLOCK]


def only(x, blocks):
    zero = jnp.zeros((BLOCK, x.shape[1]), x.dtype)
    count = x.shape[0] // BLOCK
    return jnp.concatenate([x[b * BLOCK : (b + 1) * BLOCK] if b % 4 in blocks else zero for b in range(count)], axis=0)


ALL, ODD, EVEN, LATE, FIRST = (0, 1, 2, 3), (1, 3), (0, 2), (2, 3), (0, 1)


def levels_of(x, heads, inner, outer, last, cut):
    made = [per_head_halves(x * scale, heads) for scale in (inner, outer, last)]
    made[2] = only(made[2], cut)
    return made


def level_product(hi, lo, operand):
    return folded(dot_nn(hi, operand)) + dot_nn(lo, operand[:, :LANES])


def cross_product(k_heads, r_heads, blocks):
    both = picked(k_heads[:LANES] + k_heads[LANES:], blocks)
    rows = both.shape[0]
    stacked = jnp.concatenate([both[:, :LANES], both[:, LANES:]], axis=0)
    main = dot_nt(stacked, r_heads[:, :LANES])
    return main[:rows] + main[rows:] + dot_nt(both[:, :LANES], r_heads[:, LANES:])


def phase_two(i, refs):
    at = lanes_at(i)
    r, k = refs.r[:, at].astype(F32), refs.k[:, at].astype(F32)
    v, dy = refs.v[:, at], refs.dy[:, at]
    upto, before = refs.upto[:, at], refs.before[:, at]
    heads = [refs.heads[0], refs.heads[1]]
    t = totals_of(upto)
    whole = rows_of(t)
    half = 0.5 * whole
    early_0, tail_0 = jnp.exp(before - half), jnp.exp(half - upto)
    early_1, tail_1 = jnp.exp(before), jnp.exp(whole - upto)
    zero = jnp.zeros_like(t[0])
    early_2 = early_1 * jnp.exp(rows_of([zero, zero, zero, t[2]]))
    tail_2 = tail_1 * jnp.exp(rows_of([t[1], zero, zero, zero]))
    k_heads = levels_of(k, heads, tail_0, tail_1, tail_2, FIRST)
    r_heads = levels_of(r, heads, early_0, early_1, early_2, LATE)
    dy_heads = per_head_rows(dy, heads)

    hi, lo = halves(dot_nt(dy, per_head_rows(v, heads)))
    lower, lower_1 = refs.lower[...], refs.lower_1[...]
    inner = level_product(hi * lower, lo * lower, k_heads[0]) * early_0
    rec = [inner[b * BLOCK : (b + 1) * BLOCK] for b in ALL]
    outer = level_product(picked(hi, ODD) * lower_1, picked(lo, ODD) * lower_1, k_heads[1])
    spread(rec, outer * picked(early_1, ODD), ODD)
    spread(rec, level_product(picked(hi, LATE), picked(lo, LATE), k_heads[2]) * picked(early_2, LATE), LATE)

    hi, lo = halves(dot_nt(v, dy_heads))
    upper, upper_1 = refs.upper[...], refs.upper_1[...]
    inner = level_product(hi * upper, lo * upper, r_heads[0]) * tail_0
    key = [inner[b * BLOCK : (b + 1) * BLOCK] for b in ALL]
    outer = level_product(picked(hi, EVEN) * upper_1, picked(lo, EVEN) * upper_1, r_heads[1])
    spread(key, outer * picked(tail_1, EVEN), EVEN)
    spread(key, level_product(picked(hi, FIRST), picked(lo, FIRST), r_heads[2]) * picked(tail_2, FIRST), FIRST)

    inner = jnp.where(refs.upper_f[...] > 0.0, cross_product(k_heads[0], r_heads[0], ALL), 0.0)
    cross = [inner[b * BLOCK : (b + 1) * BLOCK] for b in ALL]
    spread(cross, cross_product(k_heads[1], r_heads[1], EVEN) * refs.upper_1f[...], EVEN)
    spread(cross, cross_product(k_heads[2], r_heads[2], FIRST), FIRST)
    hi, lo = halves(jnp.concatenate(cross, axis=0))
    val = dot_nn(hi, dy_heads) + dot_nn(lo, dy_heads)

    boost = jnp.concatenate([refs.u[pl.ds(2 * i, 1), :], refs.u[pl.ds(2 * i + 1, 1), :]], axis=1)
    dy_f = dy.astype(F32)
    own_r, own_k = r * boost, k * boost
    ones = refs.ones[...]
    scalar = dot_nn(jnp.concatenate(halves(v.astype(F32) * dy_f), axis=1), ones)
    factor = dot_nn(jnp.concatenate(halves(own_r * k), axis=1), ones)
    refs.rec[:, at] = jnp.concatenate(rec, axis=0) + own_k * scalar
    refs.key[:, at] = jnp.concatenate(key, axis=0) + own_r * scalar
    refs.val[:, at] = val + factor * dy_f


def phase_three(i, refs):
    at = lanes_at(i)
    v, dy = refs.v[:, at], refs.dy[:, at]
    early, tail = refs.early[:, at], refs.tail[:, at]
    half = LANES // 2
    heads = [refs.heads[0, :half], refs.heads[1, :half]]
    state_in = per_head_halves(refs.state_in[i], heads)
    grad_in = per_head_halves(refs.grad_in[i], heads)
    grad_hi, grad_lo = grad_in[:, :LANES], grad_in[:, LANES:]
    k_hi, k_lo = halves(refs.k[:, at].astype(F32) * tail)
    both = jnp.concatenate([k_hi, k_lo], axis=1)
    rec = refs.rec[:, at] + early * folded(dot_nn(dy, state_in))
    key = refs.key[:, at] + tail * folded(dot_nn(v, grad_in))
    val = refs.val[:, at] + (dot_nt(both, jnp.concatenate([grad_hi, grad_hi], axis=1)) + dot_nt(k_hi, grad_lo))
    refs.rec_out[:, at] = rec.astype(BF16)
    refs.key_out[:, at] = key.astype(BF16)
    refs.val_out[:, at] = val.astype(BF16)


X_SIZE = 4
HOP = 5
TERM_AT, CORE_AT, X_AT, Y_AT, Z_AT, LAST_AT = 3, 10, 21, 32, 42, 50
TERM_TICKS = 4
EVERY = 2
MIDDLE_FIRST, MIDDLE_AFTER = 10, 36
EARLY = 2

OUT = ("rec_out", "key_out", "val_out", "state_grad")


def kernel(seq_size, dp_size, names, *all_refs):
    g = SimpleNamespace(**dict(zip(names, all_refs)))
    pairs = g.state.shape[0]
    half = LANES // 2
    x_size, y_size = X_SIZE, dp_size // (2 * X_SIZE)
    z, d = lax.axis_index("seq"), lax.axis_index("dp")
    c = d % 2
    x = (d // 2) % x_size
    y = d // (2 * x_size)
    last = seq_size - 1

    def chip(x_at, y_at, c_at):
        return {"dp": (y_at * x_size + x_at) * 2 + c_at}

    ways = ((g.f_hbm, g.f), (g.k_hbm, g.k), (g.v_hbm, g.v), (g.r_hbm, g.r), (g.dy_hbm, g.dy), (g.u_hbm, g.u))
    loads = [pltpu.make_async_copy(src, dst, g.load_sem.at[at]) for at, (src, dst) in enumerate(ways)]
    for load in loads:
        load.start()
    load_initial = pltpu.make_async_copy(g.initial_hbm, g.initial, g.load_sem.at[6])

    @pl.when(z == 0)
    def _():
        load_initial.start()

    barrier = pltpu.get_barrier_semaphore()
    peers = [{"seq": (z + n) % seq_size} for n in range(1, seq_size)]
    peers += [chip((x + n) % x_size, y, c) for n in range(1, x_size)]
    peers += [chip(x, (y + n) % y_size, c) for n in range(1, y_size)]
    peers += [chip(x, y, 1 - c)]
    for peer in peers:
        pl.semaphore_signal(barrier, inc=1, device_id=peer, device_id_type=pl.DeviceIdType.MESH)

    def remote(src, dst, send, recv, to):
        return pltpu.make_async_remote_copy(
            src_ref=src, dst_ref=dst, send_sem=send, recv_sem=recv, device_id=to, device_id_type=pl.DeviceIdType.MESH
        )

    def forward(j):
        to = {"seq": (z + 1) % seq_size}
        return remote(g.state_out.at[j], g.state_in.at[j], g.fs.at[0], g.fr.at[j], to)

    def backward(j):
        to = {"seq": (z + last) % seq_size}
        return remote(g.grad_out.at[j], g.grad_in.at[j], g.bs.at[0], g.br.at[j], to)

    def forward_on(j):
        g.state_out[j] = g.decay[pl.ds(j, 1), :] * g.state_in[j] + g.state[j]
        forward(j).start()

    def backward_on(j):
        g.grad_out[j] = g.decay[pl.ds(j, 1), :] * g.grad_in[j] + g.grad[j]
        backward(j).start()

    prepare(g)
    loads[0].wait()
    lax.fori_loop(0, pairs, lambda i, s: (shard_decay(i, g), s)[1], 0)
    for load in loads[1:]:
        load.wait()

    def one_step(i, carry):
        phase_one([2 * i, 2 * i + 1], g)
        return carry

    def send_first(i):
        @pl.when(z == 0)
        def _():
            g.state_in[i] = g.initial[:, lanes_at(i)]
            forward_on(i)

        @pl.when(z == last)
        def _():
            g.grad_in[i] = jnp.zeros((half, LANES), F32)
            backward_on(i)

    def start_step(i, carry):
        phase_one([2 * i, 2 * i + 1], g)
        send_first(2 * i)
        send_first(2 * i + 1)
        return carry

    def send_step(i, carry):
        send_first(i)
        return carry

    lax.fori_loop(0, EARLY, one_step, 0)

    @pl.when(z == 0)
    def _():
        load_initial.wait()

    def decay_to(n):
        return remote(g.decay, g.decays.at[z], g.ds.at[n - 1], g.dr.at[z], {"seq": (z + n) % seq_size})

    pl.semaphore_wait(barrier, len(peers))
    for n in range(1, seq_size):

        @pl.when(z + n <= last)
        def _():
            decay_to(n).start()

    lax.fori_loop(0, 2 * EARLY, send_step, 0)
    lax.fori_loop(EARLY, pairs // 2, start_step, 0)

    def core_copy():
        return remote(
            g.term.at[:, :, pl.ds(pl.multiple_of(16 * (1 - c), 16), 16)],
            g.core_in,
            g.cs.at[0],
            g.cr.at[0],
            chip(x, y, 1 - c),
        )

    def x_copy(n):
        to = (x + n) % x_size
        return remote(g.summed.at[:, to], g.x_in.at[n - 1], g.xs.at[n - 1], g.xr.at[n - 1], chip(to, y, c))

    def y_copy(n):
        to = (y + n) % y_size
        return remote(g.x_sum.at[to], g.y_in.at[n - 1], g.ys.at[n - 1], g.yr.at[n - 1], chip(x, to, c))

    def z_copy(n):
        b, hi = n % 2, n // 2
        to = 2 * c + b + 4 * hi
        return to, remote(g.y_sum.at[pl.ds(8 * b, 8)], g.z_in.at[z], g.zs.at[n], g.zr.at[z], {"seq": to})

    def last_copy():
        return remote(g.z_sum, g.z_other, g.cs.at[1], g.cr.at[1], chip(x, y, 1 - c))

    gathers = (z % 4) // 2 == c

    def make_prefix():
        g.prefix[...] = jnp.ones((pairs, LANES), F32)
        for q in range(last):

            @pl.when(q < z)
            def _():
                remote(g.decay, g.decays.at[q], g.ds.at[0], g.dr.at[q], {"seq": z}).wait_recv()
                g.prefix[...] = g.prefix[...] * g.decays[q]

    first = iota2((half // 2, LANES), 1) < half

    def make_term(i):
        t = g.prefix[pl.ds(i, 1), :] * g.grad[i]
        top, low = t[: half // 2], t[half // 2 :]
        h = 2 * i
        g.term[h // x_size, h % x_size] = jnp.where(first, top, pltpu.roll(low, half, 1))
        g.term[h // x_size, h % x_size + 1] = jnp.where(first, pltpu.roll(top, half, 1), low)

    def sum_core():
        core_copy().wait_recv()

        def one(n, carry):
            own = g.term[n // x_size, n % x_size, pl.ds(pl.multiple_of(16 * c, 16), 16)]
            g.summed[n // x_size, n % x_size] = own + g.core_in[n // x_size, n % x_size]
            return carry

        lax.fori_loop(0, x_size * y_size, one, 0)
        for n in range(1, x_size):
            x_copy(n).start()

    def sum_x():
        for n in range(1, x_size):
            x_copy(n).wait_recv()
        for at in range(y_size):
            total = g.summed[at, x]
            for n in range(1, x_size):
                total += g.x_in[n - 1, at]
            g.x_sum[at] = total
        for n in range(1, y_size):
            y_copy(n).start()

    def sum_y():
        for n in range(1, y_size):
            y_copy(n).wait_recv()
        total = g.x_sum[y]
        for n in range(1, y_size):
            total += g.y_in[n - 1]
        g.y_sum[...] = total
        for n in range(4):
            to, copy = z_copy(n)

            @pl.when(to != z)
            def _():
                copy.start()

            @pl.when(to == z)
            def _():
                g.z_in[z] = g.y_sum[pl.ds(8 * (n % 2), 8)]

    def sum_z():
        @pl.when(gathers)
        def _():
            for q in range(seq_size):

                @pl.when(z != q)
                def _():
                    remote(
                        g.y_sum.at[pl.ds(0, 8)], g.z_in.at[q], g.zs.at[0], g.zr.at[q], {"seq": q}
                    ).wait_recv()

            total = g.z_in[0]
            for q in range(1, seq_size):
                total += g.z_in[q]
            g.z_sum[...] = total
            last_copy().start()

    def finish():
        @pl.when(jnp.logical_not(gathers))
        def _():
            last_copy().wait_recv()
            g.z_sum[...] = g.z_other[...]

        total = g.z_sum[...]
        total = jnp.where(z // 4 == 1, pltpu.roll(total, half, 1), total)
        total = jnp.where(c == 1, pltpu.roll(total, LANES - half // 2, 1), total)
        g.state_grad[...] = total[:, : half // 2]

    stages = ((TERM_AT, make_prefix), (TERM_AT + TERM_TICKS, lambda: core_copy().start()), (CORE_AT, sum_core), (X_AT, sum_x), (Y_AT, sum_y), (Z_AT, sum_z), (LAST_AT, finish))
    def tick(n, carry):
        jf = n - HOP * z
        jb = n - HOP * (last - z)
        far = HOP * jnp.maximum(z, last - z)
        middle = (2 * z == last - 1) | (2 * z == last + 1)
        after = (n - MIDDLE_AFTER) // EVERY
        beat = (n - MIDDLE_AFTER) % EVERY == 0
        early_unit = middle & (n < MIDDLE_FIRST)
        late_unit = middle & (n >= MIDDLE_AFTER) & beat & (MIDDLE_FIRST + after < pairs)
        outer_unit = jnp.logical_not(middle) & beat & (n < EVERY * pairs)
        unit = jnp.where(middle, jnp.where(n < MIDDLE_FIRST, n, MIDDLE_FIRST + after), n // EVERY)
        j = jnp.where(late_unit, MIDDLE_FIRST + after, n - far)
        takes = late_unit | ((n >= far) & (n - far < jnp.where(middle, MIDDLE_FIRST, pairs)))

        @pl.when((z > 0) & (jf >= 0) & (jf < pairs))
        def _():
            forward(jf).wait_recv()

            @pl.when(z < last)
            def _():
                forward_on(jf)

        @pl.when((z < last) & (jb >= 0) & (jb < pairs))
        def _():
            backward(jb).wait_recv()

            @pl.when(z > 0)
            def _():
                backward_on(jb)

        @pl.when(early_unit | late_unit | outer_unit)
        def _():
            phase_two(unit, g)

        for at, stage in stages:
            pl.when(n == at)(stage)

        @pl.when((n >= TERM_AT) & (n < TERM_AT + TERM_TICKS))
        def _():
            for m in range(pairs // TERM_TICKS):
                make_term((n - TERM_AT) * (pairs // TERM_TICKS) + m)

        @pl.when(takes)
        def _():
            phase_three(j, g)

        return carry

    lax.fori_loop(0, HOP * last + pairs, tick, 0)

    @pl.when(z < last)
    def _():
        remote(g.state_out, g.state_in, g.fs.at[0], g.fr.at[0], {"seq": (z + 1) % seq_size}).wait_send()

    @pl.when(z > 0)
    def _():
        remote(g.grad_out, g.grad_in, g.bs.at[0], g.br.at[0], {"seq": (z + last) % seq_size}).wait_send()

    for n in range(1, seq_size):

        @pl.when(z + n <= last)
        def _():
            decay_to(n).wait_send()

    core_copy().wait_send()
    for n in range(1, x_size):
        x_copy(n).wait_send()
    for n in range(1, y_size):
        y_copy(n).wait_send()
    for n in range(4):
        to, copy = z_copy(n)

        @pl.when(to != z)
        def _():
            copy.wait_send()

    @pl.when(gathers)
    def _():
        last_copy().wait_send()


def store_kernel(count, *refs):
    ins, outs, sem = refs[:count], refs[count : 2 * count], refs[2 * count]
    puts = [pltpu.make_async_copy(ins[n], outs[n], sem.at[n]) for n in range(count)]
    for put in puts:
        put.start()
    for put in puts:
        put.wait()


def stored(arrays):
    count = len(arrays)
    return pl.pallas_call(
        functools.partial(store_kernel, count),
        out_shape=[jax.ShapeDtypeStruct(a.shape, a.dtype) for a in arrays],
        in_specs=[pl.BlockSpec(memory_space=pltpu.VMEM)] * count,
        out_specs=[pl.BlockSpec(memory_space=pl.ANY)] * count,
        scratch_shapes=[pltpu.SemaphoreType.DMA((count,))],
        compiler_params=pltpu.CompilerParams(vmem_limit_bytes=24 << 20),
    )(*arrays)


def in_hbm(array):
    return pltpu.with_memory_space_constraint(array, pltpu.HBM)


def on_device(seq_size, dp_size, r, k, v, f, u, dy, initial):
    batch, tok, width = r.shape
    heads, size = u.shape
    pairs, half = width // LANES, LANES // 2
    x_size, y_size = X_SIZE, dp_size // (2 * X_SIZE)
    dma = lambda *n: pltpu.SemaphoreType.DMA(n)
    vmem = lambda *s: pltpu.VMEM(s, F32)
    scratch = dict(
        r=pltpu.VMEM((tok, width), BF16),
        k=pltpu.VMEM((tok, width), BF16),
        v=pltpu.VMEM((tok, width), BF16),
        f=pltpu.VMEM((tok, width), BF16),
        dy=pltpu.VMEM((tok, width), BF16),
        upto=vmem(tok, width),
        before=vmem(tok, width),
        early=vmem(tok, width),
        tail=vmem(tok, width),
        rec=vmem(tok, width),
        key=vmem(tok, width),
        val=vmem(tok, width),
        state=vmem(pairs, half, LANES),
        grad=vmem(pairs, half, LANES),
        state_in=vmem(pairs, half, LANES),
        grad_in=vmem(pairs, half, LANES),
        state_out=vmem(pairs, half, LANES),
        grad_out=vmem(pairs, half, LANES),
        initial=vmem(size, width),
        u=vmem(heads, size),
        tri=pltpu.VMEM((tok, tok), BF16),
        lower=pltpu.VMEM((tok, 2 * tok), BF16),
        upper=pltpu.VMEM((tok, 2 * tok), BF16),
        upper_f=vmem(tok, 2 * tok),
        lower_1=pltpu.VMEM((tok // 2, 2 * tok), BF16),
        upper_1=pltpu.VMEM((tok // 2, 2 * tok), BF16),
        upper_1f=vmem(tok // 2, 2 * tok),
        heads=pltpu.VMEM((2, tok, LANES), BF16),
        ones=pltpu.VMEM((2 * LANES, LANES), BF16),
        decay=vmem(pairs, LANES),
        prefix=vmem(pairs, LANES),
        decays=vmem(seq_size, pairs, LANES),
        term=vmem(y_size, x_size, half // 2, LANES),
        core_in=vmem(y_size, x_size, half // 4, LANES),
        summed=vmem(y_size, x_size, half // 4, LANES),
        x_in=vmem(x_size - 1, y_size, half // 4, LANES),
        x_sum=vmem(y_size, half // 4, LANES),
        y_in=vmem(max(y_size - 1, 1), half // 4, LANES),
        y_sum=vmem(half // 4, LANES),
        z_in=vmem(seq_size, 8, LANES),
        z_sum=vmem(8, LANES),
        z_other=vmem(8, LANES),
        load_sem=dma(7),
        fs=dma(1),
        fr=dma(pairs),
        bs=dma(1),
        br=dma(pairs),
        ds=dma(seq_size),
        dr=dma(seq_size),
        cs=dma(2),
        cr=dma(2),
        xs=dma(x_size),
        xr=dma(x_size),
        ys=dma(y_size),
        yr=dma(y_size),
        zs=dma(4),
        zr=dma(seq_size),
    )
    names = ("r_hbm", "k_hbm", "v_hbm", "f_hbm", "dy_hbm", "u_hbm", "initial_hbm") + OUT + tuple(scratch)
    anywhere = pl.BlockSpec(memory_space=pl.ANY)
    inside = pl.BlockSpec(memory_space=pltpu.VMEM)
    tokens = jax.ShapeDtypeStruct((tok, width), BF16)
    outs = pl.pallas_call(
        functools.partial(kernel, seq_size, dp_size, names),
        out_shape=[tokens] * 3 + [jax.ShapeDtypeStruct((size // seq_size, half // 2), F32)],
        in_specs=[anywhere] * 7,
        out_specs=[inside] * 4,
        scratch_shapes=list(scratch.values()),
        compiler_params=pltpu.CompilerParams(vmem_limit_bytes=24 << 20, collective_id=0, has_side_effects=True),
    )(*(in_hbm(a) for a in (*(a.reshape(tok, width) for a in (r, k, v, f, dy)), u, initial.T)))
    outs = stored(outs)
    return tuple(o.reshape(batch, tok, width) for o in outs[:3]) + (outs[3].T,)


def solution(mesh):
    rows = P("dp", "seq", None)
    return jax.shard_map(
        functools.partial(on_device, mesh.shape["seq"], mesh.shape["dp"]),
        mesh=mesh,
        in_specs=(rows, rows, rows, rows, P(), rows, P()),
        out_specs=(rows, rows, rows, P("dp", "seq")),
        check_vma=False,
    )
```

time: 70.2 us -> 54.7 us (0.78)
  Pallas kernels: 64.8 us -> 53.9 us
  local copies, waits for them, and re-layouts: 4.56 us -> 0 us
    pallas_call x1, Pallas kernels: 64.8 us -> 52.8 us  [on_device(): pl.pallas_call(functools.partial(kernel, seq_size, dp_size, names), out_s...]
    unnamed x10 -> x0, local copies, waits for them, and re-layouts: 4.56 us -> none
    pallas_call x0 -> x1, Pallas kernels: none -> 1.18 us  [stored(): pl.pallas_call(functools.partial(store_kernel, count), out_shape=[jax.Sha...]
where the time goes in v2:
time: 54.7 us; the launch traced here: 54.6 us
  Pallas kernels  53.9 us (99%)
  between operations  0.64 us (1%)
    pallas_call x1, Pallas kernels, on_device(): pl.pallas_call(functools.partial(kernel, seq_size, dp_size, names), out_s...  52.8 us
    pallas_call x1, Pallas kernels, stored(): pl.pallas_call(functools.partial(store_kernel, count), out_shape=[jax.Sha...  1.18 us

profile of v2, /device:TPU:2, one launch (start us, length us, event | category | flops | bytes accessed | tf_op | source)
XLA Modules:
  0.0 54.6 jit_solution(6896099794131277589)
XLA Ops:
  0.6 52.8 %shard_map.102 = (bf16[128,2048]{1,0:T(8,128)(2,1)S(1)}, bf16[128,2048]{1,0:T(8,128)(2,1)S(1)}, bf16[128,2048]{1,0:T(8,128)(2,1)S(1)}, f32[8,32]{1,0:T(8,128)S(1)}) custom-call(bf16[128,2048]{1,0:T(8,128)(2,1)} %bitcast.10, bf16[128,2048]{1,0:T(8,128)(2,1)} %bitcast.11, bf16[128,2048]{1,0:T(8,128)(2,1)} %bitcast.12, bf16[128,2048]{1,0:T(8,128)(2,1)} %bitcast.13, ...), custom_call_target="tpu_custom_call" | custom-call | tf_op jit(solution)/shard_map/pallas_call | solution.py:665
  53.4 1.2 %shard_map.103 = (bf16[128,2048]{1,0:T(8,128)(2,1)}, bf16[128,2048]{1,0:T(8,128)(2,1)}, bf16[128,2048]{1,0:T(8,128)(2,1)}, f32[8,32]{1,0:T(8,128)}) custom-call(bf16[128,2048]{1,0:T(8,128)(2,1)S(1)} %get-tuple-element.12.refs_0_, bf16[128,2048]{1,0:T(8,128)(2,1)S(1)} %get-tuple-element.13.refs_1_, bf16[128,2048]{1,0:T(8,128)(2,1)S(1)} %get-tuple-element.14.refs_2_, ...), custom_call_target="tpu_custom_call" | custom-call | tf_op jit(solution)/shard_map/pallas_call | solution.py:581
